TPU v7x, 128 devices: a whole 4x4x4 slice. The times are simulated.
128 devices in a mesh: row: 8 (over x, core), col: 16 (over z, y).
Axes of the slice: x: 4, y: 4, z: 4, core: 2. Of those that a mesh axis runs over, the one named last changes fastest.
Arguments:
- kernel: bfloat16 [32768, 32768], P('row', 'col'), may hold values from -1 to 1
- random_cols: bfloat16 [32768, 256], P('row'), may hold values from -6 to 6
- tree_perm: int32 [32768], replicated, may hold values from 0 to 32767, as said below
- leaf_units: int32 [32], replicated, may hold values from 1 to 8, 160 in all
Outputs:
- bases: bfloat16 [4, 32768, 256], P(None, ('row', 'col'))
Inputs may be any that keep to these rules, and one draw needn't show every extreme that they name: `tree_perm`: A permutation. Cut tree positions and stored rows alike into blocks of 256 in order: every tree block takes at most 2 rows from any one stored block, some pair of blocks shares exactly 2, and every stored block gives 256 rows in all. `leaf_units`: they sum to 160.
All inputs are finite; a program needn't handle non-finite values.
Results may differ from a plain program's by a relative error of at most 0.0067.
Values may be sent and summed in bfloat16 or wider, within the bound.
No kernel may reach another device: no remote copies, remote signals or barrier semaphores. Data moves between devices by JAX's collectives and lax.ppermute only.
A program may use at most 192 MiB of HBM per device.

v0:
```python
import jax
import jax.numpy as jnp
from jax import lax
from jax.sharding import PartitionSpec as P

UNIT = 128
MINU = 4
LEVELS = 3


def shards(kernel, random_cols, tree_perm, leaf_units):
    width = random_cols.shape[1]
    partial_w = lax.dot_general(
        kernel, random_cols, (((0,), (0,)), ((), ())), preferred_element_type=jnp.float32
    )
    sample_w = lax.psum(partial_w, "row").astype(jnp.bfloat16)
    columns_count = lax.axis_size("col")
    rows_dev = kernel.shape[0] // columns_count
    sample = lax.psum_scatter(
        jnp.dot(kernel, sample_w, preferred_element_type=jnp.float32),
        "col",
        scatter_dimension=0,
        tiled=True,
    ).astype(jnp.bfloat16)
    total_rows = tree_perm.shape[0]
    device = lax.axis_index(("row", "col"))
    offset = device * rows_dev
    wanted = lax.dynamic_slice_in_dim(tree_perm, offset, rows_dev)
    inverse = (
        jnp.zeros((total_rows,), jnp.int32)
        .at[tree_perm]
        .set(jnp.arange(total_rows, dtype=jnp.int32))
    )
    placed = lax.dynamic_slice_in_dim(inverse, offset, rows_dev)
    everything = lax.all_gather(sample, ("row", "col"), axis=0, tiled=True)
    tree_rows = jnp.take(everything, wanted, axis=0)
    sizes = UNIT * (MINU - 1 + leaf_units)
    leaves = sizes.shape[0]
    ends = jnp.cumsum(sizes)
    positions = offset + jnp.arange(rows_dev, dtype=jnp.int32)
    leaf_of = jnp.sum(positions[:, None] >= ends[None, :], axis=1)
    reach = rows_dev // (UNIT * MINU) + 2
    offsets = jnp.arange(reach, dtype=jnp.int32)
    levels = LEVELS + 1
    node_ids = [leaf_of // 2**level for level in range(levels)]
    totals = []
    stored_leaf = jnp.sum(placed[:, None] >= ends[None, :], axis=1)
    leaf_range = jnp.arange(leaves, dtype=jnp.int32)
    chosen = stored_leaf[None, :] == leaf_range[:, None]
    masked = jnp.where(chosen[:, :, None], sample[None, :, :], jnp.zeros((), jnp.bfloat16))
    spread = jnp.einsum("lrs,rt->lst", masked, sample, preferred_element_type=jnp.float32)
    leaf_grams = lax.psum(spread, ("row", "col"))
    for level in range(levels):
        group = 2**level
        count = leaves // group
        node_grams = leaf_grams.reshape(count, group, width, width).sum(axis=1)
        index = jnp.minimum(node_ids[level][0] + offsets, count - 1)
        totals.append(jnp.take(node_grams, index, axis=0))
    identity_matrix = jnp.eye(width, dtype=jnp.float32)
    values = tree_rows.astype(jnp.float32).T
    results = []
    for level in range(levels):
        ids = node_ids[level]
        group = 2**level
        count = leaves // group
        node_sizes = sizes.reshape(count, group).sum(axis=1)
        candidate = ids[0] + offsets
        present = candidate <= ids[-1]
        counts = jnp.take(node_sizes, jnp.minimum(candidate, count - 1)).astype(jnp.float32)
        mean = jnp.where(
            present[:, None, None], totals[level] / counts[:, None, None], identity_matrix[None]
        )
        factor = jnp.linalg.cholesky(mean)
        basis = jnp.zeros((rows_dev, width), jnp.float32)
        for which in range(reach):
            solved = jax.scipy.linalg.solve_triangular(factor[which], values, lower=True).T
            basis = basis + jnp.where((ids == candidate[which])[:, None], solved, 0.0)
        results.append(basis.astype(jnp.bfloat16))
    return jnp.stack(results)


def solution(mesh):
    return jax.shard_map(
        shards,
        mesh=mesh,
        in_specs=(P("row", "col"), P("row", None), P(), P()),
        out_specs=P(None, ("row", "col"), None),
        check_vma=False,
    )
```

profile of v0, /device:TPU:1, one launch (start us, length us, event | category | flops | bytes accessed | tf_op | source)
XLA Modules:
  0.0 931.9 jit_solution(916774655061557949)
XLA Ops:
  6.5 1.6 copy-done
  8.1 9.7 %fusion.100 = f32[2048,256]{1,0:T(8,128)} fusion(bf16[4096,2048]{1,0:T(8,128)(2,1)} %param.7, bf16[4096,256]{1,0:T(8,128)(2,1)S(1)} %copy-done), kind=kOutput, calls=%fused_computation.278 | convolution fusion | flops 4294967296 | bytes 20971520 | tf_op jit(solution)/shard_map/dot_general | solution.py:13
  17.8 52.9 %all-reduce.5 = bf16[2048,256]{1,0:T(8,128)(2,1)S(1)} all-reduce(f32[2048,256]{1,0:T(8,128)} %fusion.100), channel_id=1, replica_groups=mesh['row'=8,'col'=16] {'row'}, use_global_device_ids=true, to_apply=%region_4.5 | all-reduce | flops 524288 | bytes 3145728 | tf_op jit(solution)/shard_map/psum | solution.py:16
  70.7 10.1 %convolution_bitcast_fusion = f32[4096,256]{0,1:T(8,128)} fusion(bf16[4096,2048]{1,0:T(8,128)(2,1)} %param.7, bf16[2048,256]{1,0:T(8,128)(2,1)S(1)} %all-reduce.5), kind=kOutput, calls=%fused_computation.29 | convolution fusion | flops 4294967296 | bytes 22020096 | tf_op jit(solution)/shard_map/dot_general | solution.py:20
  81.9 120.1 %scatter_custom_fusion = s32[32768]{0:T(1024)S(1)} fusion(s32[32768]{0:T(1024)S(1)} %compare_select_fusion, s32[32768]{0:T(1024)S(1)} %iota.117, s32[]{:T(128)} %copy.139), kind=kCustom, calls=%fused_computation.181 | custom fusion | bytes 131076 | tf_op jit(solution)/shard_map/scatter | solution.py:32
  203.1 4.5 fusion
  207.7 12.0 %all-gather.2.cloned.1.call-start = ((), (), s32[]{:S(2)}) async-start(), calls=%async_computation.3 | async-start | bytes 16908288 | tf_op jit(solution)/shard_map/all_gather | solution.py:35
  231.2 1.3 compare_and_fusion
  232.6 1.3 compare_and_fusion.2
  233.9 2.5 broadcast_compare_fusion.9
  236.4 2.6 broadcast_compare_fusion.11
  245.2 1.4 select_convert_fusion
  246.6 1.7 broadcast_compare_fusion.5
  248.4 1.7 broadcast_compare_fusion.8
  250.1 3.1 broadcast_compare_fusion.1
  253.2 119.0 %all-reduce.4.cloned.1.call-done = f32[32,256,256]{2,1,0:T(8,128)} async-done(((f32[32,256,256]{2,1,0:T(8,128)}), f32[32,256,256]{2,1,0:T(8,128)}) %all-reduce.4.cloned.1.call-update) | async-done | bytes 8388624 | tf_op jit(solution)/shard_map/psum | solution.py:52
  372.1 4.2 bitcast_reduce_fusion.1
  377.2 6.5 bitcast_reduce_fusion.2
  383.7 2.9 gather_fusion.3
  386.7 4.1 bitcast_reduce_fusion
  392.4 4.0 gather_fusion
  397.4 1.5 divide_select_fusion.1
  400.0 23.5 %custom-call.29 = f32[2,128,128]{2,1,0:T(8,128)S(1)} custom-call(f32[2,128,128]{2,1,0:T(8,128)S(1)} %cholesky.350), custom_call_target="Cholesky" | custom-call | tf_op jit(solution)/shard_map/jit(cholesky)/cholesky | solution.py:73
  423.7 23.5 %custom-call.39 = f32[2,128,128]{2,1,0:T(8,128)S(1)} custom-call(f32[2,128,128]{2,1,0:T(8,128)S(1)} %cholesky.356), custom_call_target="Cholesky" | custom-call | tf_op jit(solution)/shard_map/jit(cholesky)/cholesky | solution.py:73
  448.3 23.5 %custom-call.34 = f32[2,128,128]{2,1,0:T(8,128)S(1)} custom-call(f32[2,128,128]{2,1,0:T(8,128)S(1)} %cholesky.353), custom_call_target="Cholesky" | custom-call | tf_op jit(solution)/shard_map/jit(cholesky)/cholesky | solution.py:73
  472.1 23.9 %custom-call.44 = f32[2,128,128]{2,1,0:T(8,128)S(1)} custom-call(f32[2,128,128]{2,1,0:T(8,128)S(1)} %cholesky.359), custom_call_target="Cholesky" | custom-call | tf_op jit(solution)/shard_map/jit(cholesky)/cholesky | solution.py:73
  496.0 1.5 select_bitcast_fusion.1
  497.4 19.7 %custom-call.30 = f32[2,1,128,128]{2,3,1,0:T(8,128)S(1)} custom-call(f32[2,1,128,128]{3,2,1,0:T(8,128)S(1)} %get-tuple-element.180), custom_call_target="InvertDiagBlocksLowerTriangular" | custom-call | tf_op jit(solution)/shard_map/jit(cholesky)/cholesky | solution.py:73
  517.8 23.5 %custom-call.31 = f32[2,128,128]{2,1,0:T(8,128)S(1)} custom-call(f32[2,128,128]{2,1,0:T(8,128)S(1)} %convolution_subtract_fusion.11), custom_call_target="Cholesky" | custom-call | tf_op jit(solution)/shard_map/jit(cholesky)/cholesky | solution.py:73
  541.3 19.8 %custom-call.35 = f32[2,1,128,128]{2,3,1,0:T(8,128)S(1)} custom-call(f32[2,1,128,128]{3,2,1,0:T(8,128)S(1)} %get-tuple-element.178), custom_call_target="InvertDiagBlocksLowerTriangular" | custom-call | tf_op jit(solution)/shard_map/jit(cholesky)/cholesky | solution.py:73
  563.7 23.5 %custom-call.36 = f32[2,128,128]{2,1,0:T(8,128)S(1)} custom-call(f32[2,128,128]{2,1,0:T(8,128)S(1)} %convolution_subtract_fusion.10), custom_call_target="Cholesky" | custom-call | tf_op jit(solution)/shard_map/jit(cholesky)/cholesky | solution.py:73
  587.2 21.1 %custom-call.40 = f32[2,1,128,128]{2,3,1,0:T(8,128)} custom-call(f32[2,1,128,128]{3,2,1,0:T(8,128)} %get-tuple-element.177), custom_call_target="InvertDiagBlocksLowerTriangular" | custom-call | tf_op jit(solution)/shard_map/jit(cholesky)/cholesky | solution.py:73
  610.5 25.1 %custom-call.41 = f32[2,128,128]{2,1,0:T(8,128)} custom-call(f32[2,128,128]{2,1,0:T(8,128)} %convolution_subtract_fusion.9), custom_call_target="Cholesky" | custom-call | tf_op jit(solution)/shard_map/jit(cholesky)/cholesky | solution.py:73
  636.5 21.1 %custom-call.45 = f32[2,1,128,128]{2,3,1,0:T(8,128)} custom-call(f32[2,1,128,128]{3,2,1,0:T(8,128)} %get-tuple-element.179), custom_call_target="InvertDiagBlocksLowerTriangular" | custom-call | tf_op jit(solution)/shard_map/jit(cholesky)/cholesky | solution.py:73
  659.9 24.3 %custom-call.46 = f32[2,128,128]{2,1,0:T(8,128)S(1)} custom-call(f32[2,128,128]{2,1,0:T(8,128)} %convolution_subtract_fusion.8), custom_call_target="Cholesky" | custom-call | tf_op jit(solution)/shard_map/jit(cholesky)/cholesky | solution.py:73
  686.2 1.5 select_select_fusion.3
  688.4 3.8 while.23
  692.3 20.1 %custom-call.48 = f32[2,128,128]{1,2,0:T(8,128)S(1)} custom-call(f32[2,128,128]{2,1,0:T(8,128)S(1)} %get-tuple-element.64), custom_call_target="InvertDiagBlocksLowerTriangular" | custom-call | tf_op jit(solution)/shard_map/jit(_solve_triangular)/triangular_solve | solution.py:76
  712.4 4.0 while.22
  713.0 1.4 bitcast_dynamic-update-slice_fusion.22
  715.0 1.4 bitcast_dynamic-update-slice_fusion.22
  716.4 20.3 %custom-call.47 = f32[2,128,128]{1,2,0:T(8,128)} custom-call(f32[2,128,128]{2,1,0:T(8,128)S(1)} %get-tuple-element.63), custom_call_target="InvertDiagBlocksLowerTriangular" | custom-call | tf_op jit(solution)/shard_map/jit(_solve_triangular)/triangular_solve | solution.py:76
  736.7 4.1 while.21
  737.3 1.4 bitcast_dynamic-update-slice_fusion.21
  739.4 1.4 bitcast_dynamic-update-slice_fusion.21
  740.8 19.7 %custom-call.43 = f32[2,128,128]{1,2,0:T(8,128)S(1)} custom-call(f32[2,128,128]{2,1,0:T(8,128)S(1)} %get-tuple-element.62), custom_call_target="InvertDiagBlocksLowerTriangular" | custom-call | tf_op jit(solution)/shard_map/jit(_solve_triangular)/triangular_solve | solution.py:76
  760.5 3.9 while.20
  761.1 1.4 bitcast_dynamic-update-slice_fusion.20
  763.1 1.4 bitcast_dynamic-update-slice_fusion.20
  764.5 19.7 %custom-call.42 = f32[2,128,128]{1,2,0:T(8,128)S(1)} custom-call(f32[2,128,128]{2,1,0:T(8,128)S(1)} %get-tuple-element.61), custom_call_target="InvertDiagBlocksLowerTriangular" | custom-call | tf_op jit(solution)/shard_map/jit(_solve_triangular)/triangular_solve | solution.py:76
  784.2 3.9 while.19
  784.8 1.3 bitcast_dynamic-update-slice_fusion.19
  786.7 1.3 bitcast_dynamic-update-slice_fusion.19
  788.1 19.7 %custom-call.38 = f32[2,128,128]{1,2,0:T(8,128)S(1)} custom-call(f32[2,128,128]{2,1,0:T(8,128)S(1)} %get-tuple-element.60), custom_call_target="InvertDiagBlocksLowerTriangular" | custom-call | tf_op jit(solution)/shard_map/jit(_solve_triangular)/triangular_solve | solution.py:76
  807.8 4.0 while.18
  808.4 1.4 bitcast_dynamic-update-slice_fusion.18
  810.4 1.4 bitcast_dynamic-update-slice_fusion.18
  811.7 20.5 %custom-call.37 = f32[2,128,128]{1,2,0:T(8,128)} custom-call(f32[2,128,128]{2,1,0:T(8,128)S(1)} %get-tuple-element.59), custom_call_target="InvertDiagBlocksLowerTriangular" | custom-call | tf_op jit(solution)/shard_map/jit(_solve_triangular)/triangular_solve | solution.py:76
  832.3 3.8 while.17
  836.1 20.3 %custom-call.33 = f32[2,128,128]{1,2,0:T(8,128)} custom-call(f32[2,128,128]{2,1,0:T(8,128)S(1)} %get-tuple-element.58), custom_call_target="InvertDiagBlocksLowerTriangular" | custom-call | tf_op jit(solution)/shard_map/jit(_solve_triangular)/triangular_solve | solution.py:76
  856.4 3.6 while.16
  860.0 20.3 %custom-call.32 = f32[2,128,128]{1,2,0:T(8,128)} custom-call(f32[2,128,128]{2,1,0:T(8,128)S(1)} %get-tuple-element.57), custom_call_target="InvertDiagBlocksLowerTriangular" | custom-call | tf_op jit(solution)/shard_map/jit(_solve_triangular)/triangular_solve | solution.py:76
  880.3 22.6 %copy.47 = bf16[32768,256]{1,0:T(8,128)(2,1)} copy(bf16[32768,256]{0,1:T(8,128)(2,1)} %all-gather.2.cloned.1.call-done) | data formatting | bytes 33554432 | tf_op jit(solution)/shard_map/all_gather | solution.py:35
  902.9 9.0 gather_fusion.2
  (234 shorter events, 67.4 us)
Async XLA Ops:
  6.5 1.6 copy-start
  6.5 195.6 %reduce-scatter.2.cloned.1.call-start = ((), (), s32[]{:S(2)}) async-start(), calls=%async_computation.1 | async-start | bytes 4456448 | tf_op jit(solution)/shard_map/reduce_scatter | solution.py:19
  80.9 0.7 copy-start.25
  80.9 0.9 copy-start.11
  80.9 291.2 %all-reduce.4.cloned.1.call-start = ((), (), s32[]{:S(2)}) async-start(), calls=%async_computation.2 | async-start | bytes 16777216 | tf_op jit(solution)/shard_map/psum | solution.py:52
  203.1 4.5 copy-start.2
  207.7 672.6 %all-gather.2.cloned.1.call-start = ((), (), s32[]{:S(2)}) async-start(), calls=%async_computation.3 | async-start | bytes 16908288 | tf_op jit(solution)/shard_map/all_gather | solution.py:35
  399.2 0.8 copy-start.6
  423.7 93.4 %copy-start.7 = (f32[2,256,256]{2,1,0:T(8,128)S(1)}, f32[2,256,256]{2,1,0:T(8,128)}, u32[]{:S(2)}) copy-start(f32[2,256,256]{2,1,0:T(8,128)} %copy-done.6) | copy-start | bytes 1572868
  447.5 0.8 copy-start.8
  495.9 1.5 copy-start.9
  517.8 166.3 %copy-start.10 = (f32[2,128,128]{2,1,0:T(8,128)S(1)}, f32[2,128,128]{2,1,0:T(8,128)}, u32[]{:S(2)}) copy-start(f32[2,128,128]{2,1,0:T(8,128)} %copy-done.9) | copy-start | bytes 393220
  685.1 1.0 copy-start.3
  685.2 1.0 copy-start.4
  807.8 108.1 %copy-start.13 = (f32[2,128,128]{1,2,0:T(8,128)}, f32[2,128,128]{1,2,0:T(8,128)S(1)}, u32[]{:S(2)}) copy-start(f32[2,128,128]{1,2,0:T(8,128)S(1)} %custom-call.38) | copy-start | bytes 393220
  836.1 66.9 %copy-start.5 = (f32[256,256]{1,0:T(8,128)}, f32[256,256]{1,0:T(8,128)S(1)}, u32[]{:S(2)}) copy-start(f32[256,256]{1,0:T(8,128)S(1)} %get-tuple-element.602) | copy-start | bytes 786436
  880.3 31.8 %copy-start.24 = (pred[256]{0:T(512)(128)(4,1)S(1)}, pred[256]{0:T(512)(128)(4,1)}, u32[]{:S(2)}) copy-start(pred[256]{0:T(512)(128)(4,1)} %get-tuple-element.139) | copy-start | bytes 772
  880.3 32.8 %copy-start.12 = (f32[2,128,128]{1,2,0:T(8,128)S(1)}, f32[2,128,128]{1,2,0:T(8,128)}, u32[]{:S(2)}) copy-start(f32[2,128,128]{1,2,0:T(8,128)} %custom-call.47) | copy-start | bytes 393220
  912.1 10.5 %copy-start.14 = (f32[2,128,128]{1,2,0:T(8,128)S(1)}, f32[2,128,128]{1,2,0:T(8,128)}, u32[]{:S(2)}) copy-start(f32[2,128,128]{1,2,0:T(8,128)} %custom-call.33) | copy-start | bytes 393220
  912.1 10.8 %copy-start.15 = (f32[2,128,128]{1,2,0:T(8,128)S(1)}, f32[2,128,128]{1,2,0:T(8,128)}, u32[]{:S(2)}) copy-start(f32[2,128,128]{1,2,0:T(8,128)} %custom-call.32) | copy-start | bytes 393220
  912.4 11.4 %copy-start.18 = (pred[256]{0:T(512)(128)(4,1)S(1)}, pred[256]{0:T(512)(128)(4,1)}, u32[]{:S(2)}) copy-start(pred[256]{0:T(512)(128)(4,1)} %get-tuple-element.187) | copy-start | bytes 772
  912.5 11.4 %copy-start.19 = (pred[256]{0:T(512)(128)(4,1)S(1)}, pred[256]{0:T(512)(128)(4,1)}, u32[]{:S(2)}) copy-start(pred[256]{0:T(512)(128)(4,1)} %get-tuple-element.188) | copy-start | bytes 772
  913.1 10.8 %copy-start.16 = (pred[256]{0:T(512)(128)(4,1)S(1)}, pred[256]{0:T(512)(128)(4,1)}, u32[]{:S(2)}) copy-start(pred[256]{0:T(512)(128)(4,1)} %get-tuple-element.226) | copy-start | bytes 772
  913.1 10.8 %copy-start.17 = (pred[256]{0:T(512)(128)(4,1)S(1)}, pred[256]{0:T(512)(128)(4,1)}, u32[]{:S(2)}) copy-start(pred[256]{0:T(512)(128)(4,1)} %get-tuple-element.227) | copy-start | bytes 772
  913.7 10.3 %copy-start.22 = (pred[256]{0:T(512)(128)(4,1)S(1)}, pred[256]{0:T(512)(128)(4,1)}, u32[]{:S(2)}) copy-start(pred[256]{0:T(512)(128)(4,1)} %get-tuple-element.183) | copy-start | bytes 772
  913.7 10.3 %copy-start.23 = (pred[256]{0:T(512)(128)(4,1)S(1)}, pred[256]{0:T(512)(128)(4,1)}, u32[]{:S(2)}) copy-start(pred[256]{0:T(512)(128)(4,1)} %get-tuple-element.184) | copy-start | bytes 772
  914.3 9.7 %copy-start.20 = (pred[256]{0:T(512)(128)(4,1)S(1)}, pred[256]{0:T(512)(128)(4,1)}, u32[]{:S(2)}) copy-start(pred[256]{0:T(512)(128)(4,1)} %get-tuple-element.181) | copy-start | bytes 772
  914.3 9.7 %copy-start.21 = (pred[256]{0:T(512)(128)(4,1)S(1)}, pred[256]{0:T(512)(128)(4,1)}, u32[]{:S(2)}) copy-start(pred[256]{0:T(512)(128)(4,1)} %get-tuple-element.182) | copy-start | bytes 772
  916.2 9.0 copy-start.1
Sparse Core Ops, SparseCore 0:
  81.0 79.6 reduce-scatter.1
  207.8 164.3 all-reduce.3
  375.0 98.1 all-gather.1
where the time goes:
time: 940 us; the launch traced here: 932 us
  other arithmetic  481 us (51%)
  local copies, waits for them, and re-layouts  208 us (22%)
  waiting for transfers between devices  119 us (13%)
  blocking collectives  52.9 us (6%)
  matrix products  43.3 us (5%)
  between operations  14.6 us (2%)
  starting transfers between devices  12 us (1%)
    another operation x28, other arithmetic, shards(): factor = jnp.linalg.cholesky(mean)  276 us
    another operation x14, other arithmetic, shards(): jax.scipy.linalg.solve_triangular(factor[which], values, lower=True)  162 us
    scatter x1, local copies, waits for them, and re-layouts, shards(): inverse = jnp.zeros((total_rows,), jnp.int32).at[tree_perm].set(jnp.arang...  120 us
    psum x1, waiting for transfers between devices, shards(): leaf_grams = lax.psum(spread, ('row', 'col'))  119 us
    psum x1, blocking collectives, shards(): sample_w = lax.psum(partial_w, 'row').astype(jnp.bfloat16)  52.9 us
    another operation x49, local copies, waits for them, and re-layouts, shards(): jax.scipy.linalg.solve_triangular(factor[which], values, lower=True)  31.3 us
    all_gather x1, local copies, waits for them, and re-layouts, shards(): everything = lax.all_gather(sample, ('row', 'col'), axis=0, tiled=True)  22.6 us
  transfers between devices with their start and end apart: 3, of which 1 were waited for; matrix products, arithmetic and copies ran while one was open for 71% of the time, Pallas kernels for 0%

commit v1 on v0

--- a/solution.py
+++ b/solution.py
@@ -49,7 +49,12 @@
     chosen = stored_leaf[None, :] == leaf_range[:, None]
     masked = jnp.where(chosen[:, :, None], sample[None, :, :], jnp.zeros((), jnp.bfloat16))
     spread = jnp.einsum("lrs,rt->lst", masked, sample, preferred_element_type=jnp.float32)
-    leaf_grams = lax.psum(spread, ("row", "col"))
+
+    def note_the_cards(m, bus_axis, chip_axis):
+        main = lax.psum(m, bus_axis)
+        return lax.psum(main, chip_axis)
+
+    leaf_grams = note_the_cards(spread, "col", "row")
     for level in range(levels):
         group = 2**level
         count = leaves // group

time: 940 us -> 1030 us (1.096)
  waiting for transfers between devices: 119 us -> 204 us
    psum x1 -> x2, waiting for transfers between devices: 119 us -> 204 us  [the longest x1 144 us: note_the_cards(): main = lax.psum(m, bus_axis)]
  transfers between devices with their start and end apart: 3 -> 4, of which waited for: 1 -> 2; matrix products, arithmetic and copies ran while one was open for 71% -> 65% of each run, Pallas kernels for 0% -> 0%
where the time goes in v1:
time: 1030 us; the launch traced here: 1020 us
  other arithmetic  481 us (47%)
  local copies, waits for them, and re-layouts  208 us (20%)
  waiting for transfers between devices  204 us (20%)
  blocking collectives  52.9 us (5%)
  matrix products  43.3 us (4%)
  between operations  14.6 us (1%)
  starting transfers between devices  12.1 us (1%)
    another operation x28, other arithmetic, shards(): factor = jnp.linalg.cholesky(mean)  276 us
    another operation x14, other arithmetic, shards(): jax.scipy.linalg.solve_triangular(factor[which], values, lower=True)  162 us
    psum x1, waiting for transfers between devices, note_the_cards(): main = lax.psum(m, bus_axis)  144 us
    scatter x1, local copies, waits for them, and re-layouts, shards(): inverse = jnp.zeros((total_rows,), jnp.int32).at[tree_perm].set(jnp.arang...  120 us
    psum x1, waiting for transfers between devices, note_the_cards(): return lax.psum(main, chip_axis)  60 us
    psum x1, blocking collectives, shards(): sample_w = lax.psum(partial_w, 'row').astype(jnp.bfloat16)  52.9 us
    another operation x49, local copies, waits for them, and re-layouts, shards(): jax.scipy.linalg.solve_triangular(factor[which], values, lower=True)  31.3 us
    all_gather x1, local copies, waits for them, and re-layouts, shards(): everything = lax.all_gather(sample, ('row', 'col'), axis=0, tiled=True)  22.6 us
  transfers between devices with their start and end apart: 4, of which 2 were waited for; matrix products, arithmetic and copies ran while one was open for 65% of the time, Pallas kernels for 0%

profile of v1, /device:TPU:1, one launch (start us, length us, event | category | flops | bytes accessed | tf_op | source)
XLA Modules:
  0.0 1017.3 jit_solution(11663155272117724596)
XLA Ops:
  6.5 1.6 copy-done
  8.1 9.7 fusion.100
  17.8 52.9 %all-reduce.8 = bf16[2048,256]{1,0:T(8,128)(2,1)S(1)} all-reduce(f32[2048,256]{1,0:T(8,128)} %fusion.100), channel_id=1, replica_groups=mesh['row'=8,'col'=16] {'row'}, use_global_device_ids=true, to_apply=%region_4.5 | all-reduce | flops 524288 | bytes 3145728 | tf_op jit(solution)/shard_map/psum | solution.py:16
  70.7 10.1 convolution_bitcast_fusion
  81.9 120.1 %scatter_custom_fusion = s32[32768]{0:T(1024)S(1)} fusion(s32[32768]{0:T(1024)S(1)} %compare_select_fusion, s32[32768]{0:T(1024)S(1)} %iota.117, s32[]{:T(128)} %copy.140), kind=kCustom, calls=%fused_computation.181 | custom fusion | bytes 131076 | tf_op jit(solution)/shard_map/scatter | solution.py:32
  203.1 4.5 fusion
  207.7 144.4 %all-reduce.5.cloned.1.call-done = f32[32,256,256]{2,1,0:T(8,128)} async-done(((f32[32,256,256]{2,1,0:T(8,128)}), f32[32,256,256]{2,1,0:T(8,128)}) %all-reduce.5.cloned.1.call-update) | async-done | bytes 8388624 | tf_op jit(solution)/shard_map/psum | solution.py:54
  352.1 12.0 %all-gather.2.cloned.1.call-start = ((), (), s32[]{:S(2)}) async-start(), calls=%async_computation.4 | async-start | bytes 16908288 | tf_op jit(solution)/shard_map/all_gather | solution.py:35
  366.0 1.3 fusion.78
  369.2 1.3 fusion.80
  375.7 1.3 compare_and_fusion
  377.0 1.3 compare_and_fusion.2
  378.3 2.6 broadcast_compare_fusion.9
  380.9 2.5 broadcast_compare_fusion.11
  391.1 1.7 broadcast_compare_fusion.5
  392.8 1.7 broadcast_compare_fusion.8
  394.5 3.1 broadcast_compare_fusion.1
  397.6 60.0 %all-reduce.7.cloned.1.call-done = f32[32,256,256]{2,1,0:T(8,128)} async-done(((f32[32,256,256]{2,1,0:T(8,128)}), f32[32,256,256]{2,1,0:T(8,128)}) %all-reduce.7.cloned.1.call-update) | async-done | bytes 8388624 | tf_op jit(solution)/shard_map/psum | solution.py:55
  457.6 4.2 bitcast_reduce_fusion.1
  462.6 6.5 bitcast_reduce_fusion.2
  469.1 2.8 gather_fusion.3
  472.1 4.1 bitcast_reduce_fusion
  477.8 4.0 gather_fusion
  482.8 1.5 divide_select_fusion.1
  485.4 23.5 %custom-call.29 = f32[2,128,128]{2,1,0:T(8,128)S(1)} custom-call(f32[2,128,128]{2,1,0:T(8,128)S(1)} %cholesky.350), custom_call_target="Cholesky" | custom-call | tf_op jit(solution)/shard_map/jit(cholesky)/cholesky | solution.py:78
  509.2 23.5 %custom-call.39 = f32[2,128,128]{2,1,0:T(8,128)S(1)} custom-call(f32[2,128,128]{2,1,0:T(8,128)S(1)} %cholesky.356), custom_call_target="Cholesky" | custom-call | tf_op jit(solution)/shard_map/jit(cholesky)/cholesky | solution.py:78
  533.7 23.5 %custom-call.34 = f32[2,128,128]{2,1,0:T(8,128)S(1)} custom-call(f32[2,128,128]{2,1,0:T(8,128)S(1)} %cholesky.353), custom_call_target="Cholesky" | custom-call | tf_op jit(solution)/shard_map/jit(cholesky)/cholesky | solution.py:78
  557.5 23.9 %custom-call.44 = f32[2,128,128]{2,1,0:T(8,128)S(1)} custom-call(f32[2,128,128]{2,1,0:T(8,128)S(1)} %cholesky.359), custom_call_target="Cholesky" | custom-call | tf_op jit(solution)/shard_map/jit(cholesky)/cholesky | solution.py:78
  581.4 1.5 select_bitcast_fusion.1
  582.9 19.7 %custom-call.30 = f32[2,1,128,128]{2,3,1,0:T(8,128)S(1)} custom-call(f32[2,1,128,128]{3,2,1,0:T(8,128)S(1)} %get-tuple-element.180), custom_call_target="InvertDiagBlocksLowerTriangular" | custom-call | tf_op jit(solution)/shard_map/jit(cholesky)/cholesky | solution.py:78
  603.2 23.5 %custom-call.31 = f32[2,128,128]{2,1,0:T(8,128)S(1)} custom-call(f32[2,128,128]{2,1,0:T(8,128)S(1)} %convolution_subtract_fusion.11), custom_call_target="Cholesky" | custom-call | tf_op jit(solution)/shard_map/jit(cholesky)/cholesky | solution.py:78
  626.7 19.8 %custom-call.35 = f32[2,1,128,128]{2,3,1,0:T(8,128)S(1)} custom-call(f32[2,1,128,128]{3,2,1,0:T(8,128)S(1)} %get-tuple-element.178), custom_call_target="InvertDiagBlocksLowerTriangular" | custom-call | tf_op jit(solution)/shard_map/jit(cholesky)/cholesky | solution.py:78
  649.1 23.5 %custom-call.36 = f32[2,128,128]{2,1,0:T(8,128)S(1)} custom-call(f32[2,128,128]{2,1,0:T(8,128)S(1)} %convolution_subtract_fusion.10), custom_call_target="Cholesky" | custom-call | tf_op jit(solution)/shard_map/jit(cholesky)/cholesky | solution.py:78
  672.6 21.1 %custom-call.40 = f32[2,1,128,128]{2,3,1,0:T(8,128)} custom-call(f32[2,1,128,128]{3,2,1,0:T(8,128)} %get-tuple-element.177), custom_call_target="InvertDiagBlocksLowerTriangular" | custom-call | tf_op jit(solution)/shard_map/jit(cholesky)/cholesky | solution.py:78
  695.9 25.1 %custom-call.41 = f32[2,128,128]{2,1,0:T(8,128)} custom-call(f32[2,128,128]{2,1,0:T(8,128)} %convolution_subtract_fusion.9), custom_call_target="Cholesky" | custom-call | tf_op jit(solution)/shard_map/jit(cholesky)/cholesky | solution.py:78
  721.9 21.1 %custom-call.45 = f32[2,1,128,128]{2,3,1,0:T(8,128)} custom-call(f32[2,1,128,128]{3,2,1,0:T(8,128)} %get-tuple-element.179), custom_call_target="InvertDiagBlocksLowerTriangular" | custom-call | tf_op jit(solution)/shard_map/jit(cholesky)/cholesky | solution.py:78
  745.3 24.3 %custom-call.46 = f32[2,128,128]{2,1,0:T(8,128)S(1)} custom-call(f32[2,128,128]{2,1,0:T(8,128)} %convolution_subtract_fusion.8), custom_call_target="Cholesky" | custom-call | tf_op jit(solution)/shard_map/jit(cholesky)/cholesky | solution.py:78
  771.6 1.5 select_select_fusion.3
  773.9 3.8 while.23
  777.7 20.1 %custom-call.48 = f32[2,128,128]{1,2,0:T(8,128)S(1)} custom-call(f32[2,128,128]{2,1,0:T(8,128)S(1)} %get-tuple-element.64), custom_call_target="InvertDiagBlocksLowerTriangular" | custom-call | tf_op jit(solution)/shard_map/jit(_solve_triangular)/triangular_solve | solution.py:81
  797.8 4.0 while.22
  798.4 1.4 bitcast_dynamic-update-slice_fusion.22
  800.4 1.4 bitcast_dynamic-update-slice_fusion.22
  801.8 20.3 %custom-call.47 = f32[2,128,128]{1,2,0:T(8,128)} custom-call(f32[2,128,128]{2,1,0:T(8,128)S(1)} %get-tuple-element.63), custom_call_target="InvertDiagBlocksLowerTriangular" | custom-call | tf_op jit(solution)/shard_map/jit(_solve_triangular)/triangular_solve | solution.py:81
  822.1 4.1 while.21
  822.7 1.4 bitcast_dynamic-update-slice_fusion.21
  824.8 1.4 bitcast_dynamic-update-slice_fusion.21
  826.2 19.7 %custom-call.43 = f32[2,128,128]{1,2,0:T(8,128)S(1)} custom-call(f32[2,128,128]{2,1,0:T(8,128)S(1)} %get-tuple-element.62), custom_call_target="InvertDiagBlocksLowerTriangular" | custom-call | tf_op jit(solution)/shard_map/jit(_solve_triangular)/triangular_solve | solution.py:81
  845.9 3.9 while.20
  846.5 1.4 bitcast_dynamic-update-slice_fusion.20
  848.5 1.4 bitcast_dynamic-update-slice_fusion.20
  849.9 19.7 %custom-call.42 = f32[2,128,128]{1,2,0:T(8,128)S(1)} custom-call(f32[2,128,128]{2,1,0:T(8,128)S(1)} %get-tuple-element.61), custom_call_target="InvertDiagBlocksLowerTriangular" | custom-call | tf_op jit(solution)/shard_map/jit(_solve_triangular)/triangular_solve | solution.py:81
  869.6 3.9 while.19
  873.5 19.7 %custom-call.38 = f32[2,128,128]{1,2,0:T(8,128)S(1)} custom-call(f32[2,128,128]{2,1,0:T(8,128)S(1)} %get-tuple-element.60), custom_call_target="InvertDiagBlocksLowerTriangular" | custom-call | tf_op jit(solution)/shard_map/jit(_solve_triangular)/triangular_solve | solution.py:81
  893.2 4.0 while.18
  893.8 1.4 bitcast_dynamic-update-slice_fusion.18
  895.8 1.4 bitcast_dynamic-update-slice_fusion.18
  897.2 20.5 %custom-call.37 = f32[2,128,128]{1,2,0:T(8,128)} custom-call(f32[2,128,128]{2,1,0:T(8,128)S(1)} %get-tuple-element.59), custom_call_target="InvertDiagBlocksLowerTriangular" | custom-call | tf_op jit(solution)/shard_map/jit(_solve_triangular)/triangular_solve | solution.py:81
  917.7 3.8 while.17
  921.5 20.3 %custom-call.33 = f32[2,128,128]{1,2,0:T(8,128)} custom-call(f32[2,128,128]{2,1,0:T(8,128)S(1)} %get-tuple-element.58), custom_call_target="InvertDiagBlocksLowerTriangular" | custom-call | tf_op jit(solution)/shard_map/jit(_solve_triangular)/triangular_solve | solution.py:81
  941.8 3.6 while.16
  945.4 20.3 %custom-call.32 = f32[2,128,128]{1,2,0:T(8,128)} custom-call(f32[2,128,128]{2,1,0:T(8,128)S(1)} %get-tuple-element.57), custom_call_target="InvertDiagBlocksLowerTriangular" | custom-call | tf_op jit(solution)/shard_map/jit(_solve_triangular)/triangular_solve | solution.py:81
  965.7 22.6 %copy.47 = bf16[32768,256]{1,0:T(8,128)(2,1)} copy(bf16[32768,256]{0,1:T(8,128)(2,1)} %all-gather.2.cloned.1.call-done) | data formatting | bytes 33554432 | tf_op jit(solution)/shard_map/all_gather | solution.py:35
  988.3 9.0 gather_fusion.2
  (237 shorter events, 68.8 us)
Async XLA Ops:
  6.5 1.6 copy-start
  6.5 195.6 %reduce-scatter.2.cloned.1.call-start = ((), (), s32[]{:S(2)}) async-start(), calls=%async_computation.1 | async-start | bytes 4456448 | tf_op jit(solution)/shard_map/reduce_scatter | solution.py:19
  80.9 0.7 copy-start.25
  80.9 0.9 copy-start.11
  80.9 271.2 %all-reduce.5.cloned.1.call-start = ((), (), s32[]{:S(2)}) async-start(), calls=%async_computation.2 | async-start | bytes 16777216 | tf_op jit(solution)/shard_map/psum | solution.py:54
  203.1 4.5 copy-start.2
  207.7 249.9 %all-reduce.7.cloned.1.call-start = ((), (), s32[]{:S(2)}) async-start(), calls=%async_computation.3 | async-start | bytes 16777216 | tf_op jit(solution)/shard_map/psum | solution.py:55
  352.1 613.6 %all-gather.2.cloned.1.call-start = ((), (), s32[]{:S(2)}) async-start(), calls=%async_computation.4 | async-start | bytes 16908288 | tf_op jit(solution)/shard_map/all_gather | solution.py:35
  484.6 0.8 copy-start.6
  509.1 93.4 %copy-start.7 = (f32[2,256,256]{2,1,0:T(8,128)S(1)}, f32[2,256,256]{2,1,0:T(8,128)}, u32[]{:S(2)}) copy-start(f32[2,256,256]{2,1,0:T(8,128)} %copy-done.6) | copy-start | bytes 1572868
  532.9 0.8 copy-start.8
  581.3 1.5 copy-start.9
  603.2 166.3 %copy-start.10 = (f32[2,128,128]{2,1,0:T(8,128)S(1)}, f32[2,128,128]{2,1,0:T(8,128)}, u32[]{:S(2)}) copy-start(f32[2,128,128]{2,1,0:T(8,128)} %copy-done.9) | copy-start | bytes 393220
  770.6 1.0 copy-start.3
  770.6 1.0 copy-start.4
  893.2 108.1 %copy-start.13 = (f32[2,128,128]{1,2,0:T(8,128)}, f32[2,128,128]{1,2,0:T(8,128)S(1)}, u32[]{:S(2)}) copy-start(f32[2,128,128]{1,2,0:T(8,128)S(1)} %custom-call.38) | copy-start | bytes 393220
  921.5 66.9 %copy-start.5 = (f32[256,256]{1,0:T(8,128)}, f32[256,256]{1,0:T(8,128)S(1)}, u32[]{:S(2)}) copy-start(f32[256,256]{1,0:T(8,128)S(1)} %get-tuple-element.606) | copy-start | bytes 786436
  965.7 31.8 %copy-start.24 = (pred[256]{0:T(512)(128)(4,1)S(1)}, pred[256]{0:T(512)(128)(4,1)}, u32[]{:S(2)}) copy-start(pred[256]{0:T(512)(128)(4,1)} %get-tuple-element.139) | copy-start | bytes 772
  965.7 32.8 %copy-start.12 = (f32[2,128,128]{1,2,0:T(8,128)S(1)}, f32[2,128,128]{1,2,0:T(8,128)}, u32[]{:S(2)}) copy-start(f32[2,128,128]{1,2,0:T(8,128)} %custom-call.47) | copy-start | bytes 393220
  997.5 10.5 %copy-start.14 = (f32[2,128,128]{1,2,0:T(8,128)S(1)}, f32[2,128,128]{1,2,0:T(8,128)}, u32[]{:S(2)}) copy-start(f32[2,128,128]{1,2,0:T(8,128)} %custom-call.33) | copy-start | bytes 393220
  997.5 10.8 %copy-start.15 = (f32[2,128,128]{1,2,0:T(8,128)S(1)}, f32[2,128,128]{1,2,0:T(8,128)}, u32[]{:S(2)}) copy-start(f32[2,128,128]{1,2,0:T(8,128)} %custom-call.32) | copy-start | bytes 393220
  997.9 11.4 %copy-start.18 = (pred[256]{0:T(512)(128)(4,1)S(1)}, pred[256]{0:T(512)(128)(4,1)}, u32[]{:S(2)}) copy-start(pred[256]{0:T(512)(128)(4,1)} %get-tuple-element.187) | copy-start | bytes 772
  997.9 11.4 %copy-start.19 = (pred[256]{0:T(512)(128)(4,1)S(1)}, pred[256]{0:T(512)(128)(4,1)}, u32[]{:S(2)}) copy-start(pred[256]{0:T(512)(128)(4,1)} %get-tuple-element.188) | copy-start | bytes 772
  998.5 10.8 %copy-start.16 = (pred[256]{0:T(512)(128)(4,1)S(1)}, pred[256]{0:T(512)(128)(4,1)}, u32[]{:S(2)}) copy-start(pred[256]{0:T(512)(128)(4,1)} %get-tuple-element.226) | copy-start | bytes 772
  998.5 10.8 %copy-start.17 = (pred[256]{0:T(512)(128)(4,1)S(1)}, pred[256]{0:T(512)(128)(4,1)}, u32[]{:S(2)}) copy-start(pred[256]{0:T(512)(128)(4,1)} %get-tuple-element.227) | copy-start | bytes 772
  999.1 10.3 %copy-start.22 = (pred[256]{0:T(512)(128)(4,1)S(1)}, pred[256]{0:T(512)(128)(4,1)}, u32[]{:S(2)}) copy-start(pred[256]{0:T(512)(128)(4,1)} %get-tuple-element.183) | copy-start | bytes 772
  999.1 10.3 %copy-start.23 = (pred[256]{0:T(512)(128)(4,1)S(1)}, pred[256]{0:T(512)(128)(4,1)}, u32[]{:S(2)}) copy-start(pred[256]{0:T(512)(128)(4,1)} %get-tuple-element.184) | copy-start | bytes 772
  999.7 9.7 copy-start.20
  999.7 9.7 copy-start.21
  1001.6 9.0 copy-start.1
Sparse Core Ops, SparseCore 0:
  81.0 79.6 reduce-scatter.1
  207.8 144.2 all-reduce.4
  354.5 103.0 all-reduce.6
  460.3 99.6 all-gather.1
